TPU v7x, 32 devices: a whole 2x2x4 slice. The times are simulated.
32 devices in a mesh: gz: 2 (over core), dp: 16 (over z, y, x).
Axes of the slice: x: 2, y: 2, z: 4, core: 2. Of those that a mesh axis runs over, the one named last changes fastest.
Arguments:
- inputs: bfloat16 [16, 32, 16, 8, 128], P('dp', None, 'gz'), may hold values from -6 to 6
- kernel_one: bfloat16 [32, 32, 3, 3, 3], replicated, may hold values from -0.21875 to 0.21875
- kernel_two: bfloat16 [32, 32, 3, 3, 3], replicated, may hold values from -0.21875 to 0.21875
- cotangent: bfloat16 [16, 32, 16, 8, 128], P('dp', None, 'gz'), may hold values from -12 to 12
Outputs:
- input_grad: bfloat16 [16, 32, 16, 8, 128], P('dp', None, 'gz')
- kernel_one_grad: float32 [32, 32, 3, 3, 3], replicated
- kernel_two_grad: float32 [32, 32, 3, 3, 3], replicated
All inputs are finite; a program needn't handle non-finite values.
Results may differ from a plain program's by a relative error of at most 0.006.
Values may be sent and summed in bfloat16 or wider, within the bound.
A program may use at most 64 MiB of HBM per device.

v0:
```python
import math

import jax
import jax.numpy as jnp
from jax import lax
from jax.sharding import PartitionSpec as P


def extended(value, sides, width):
    for axis, dim in sides:
        count, length = (lax.axis_size(axis), value.shape[dim])
        up = [(i, (i + 1) % count) for i in range(count - 1)]
        down = [(j, i) for i, j in up]
        last = lax.slice_in_dim(value, length - width, length, axis=dim)
        initial = lax.slice_in_dim(value, 0, width, axis=dim)
        before = lax.ppermute(last, axis, up)
        after = lax.ppermute(initial, axis, down)
        value = jnp.concatenate([before, value, after], axis=dim)
    return value


def column_stack(field):
    padded = jnp.pad(field, ((0, 0), (0, 0), (1, 1), (1, 1)))
    width = field.shape[3]
    return jnp.stack([padded[..., col_off : col_off + width] for col_off in range(3)])


def convolve_valid(field, kernel):
    stacked = column_stack(field)
    planes = field.shape[1] - 2
    height = field.shape[2]
    total = None
    for plane_off in range(3):
        for row_off in range(3):
            weights = jnp.moveaxis(kernel[:, :, plane_off, row_off, :], 2, 1)
            window = stacked[:, :, plane_off : plane_off + planes, row_off : row_off + height, :]
            piece = jnp.einsum(
                "oki,kizyx->ozyx", weights, window, preferred_element_type=jnp.float32
            )
            total = piece if total is None else total + piece
    return total


def convolve_all(fields, kernel):
    return jax.vmap(convolve_valid, in_axes=(0, None))(fields, kernel)


def flipped(kernel):
    return jnp.swapaxes(jnp.flip(kernel, (2, 3, 4)), 0, 1)


def kernel_terms(banded, grad):
    stacked = column_stack(banded)
    planes = grad.shape[1]
    height = grad.shape[2]
    outer = []
    for plane_off in range(3):
        inner = []
        for row_off in range(3):
            window = stacked[:, :, plane_off : plane_off + planes, row_off : row_off + height, :]
            inner.append(
                jnp.einsum("ozyx,kizyx->oik", grad, window, preferred_element_type=jnp.float32)
            )
        outer.append(jnp.stack(inner, 2))
    return jnp.stack(outer, 2)


def terms_all(banded, grad):
    return jnp.sum(jax.vmap(kernel_terms)(banded, grad), axis=0)


def dsilu(value):
    sigmoid_val = jax.nn.sigmoid(value)
    return sigmoid_val * (1.0 + value * (1.0 - sigmoid_val))


def local(inputs, kernel_one, kernel_two, cotangent):
    slab_depth = inputs.shape[2]
    source_band = extended(inputs, (("gz", 2),), 1)
    pre_one = convolve_all(source_band, kernel_one)
    hidden = jax.nn.silu(pre_one).astype(jnp.bfloat16)
    hidden_band = extended(hidden, (("gz", 2),), 1)
    pre_two = convolve_all(hidden_band, kernel_two)
    grad_two = (cotangent.astype(jnp.float32) * dsilu(pre_two)).astype(jnp.bfloat16)
    grad_two_band = extended(grad_two, (("gz", 2),), 1)
    hidden_grad = convolve_all(grad_two_band, flipped(kernel_two))
    grad_one = (hidden_grad * dsilu(pre_one)).astype(jnp.bfloat16)
    grad_one_band = extended(grad_one, (("gz", 2),), 1)
    input_grad = convolve_all(grad_one_band, flipped(kernel_one)).astype(jnp.bfloat16)
    term_two = terms_all(hidden_band, grad_two)
    term_one = terms_all(source_band, grad_one)
    total_one, total_two = lax.psum((term_one, term_two), ("gz", "dp"))
    count = (
        lax.axis_size("dp")
        * inputs.shape[0]
        * lax.axis_size("gz")
        * slab_depth
        * inputs.shape[3]
        * inputs.shape[4]
    )
    factor = 1.0 / math.sqrt(count)
    return (input_grad, total_one * factor, total_two * factor)


def solution(mesh):
    return jax.shard_map(
        local,
        mesh=mesh,
        in_specs=(P("dp", None, "gz", None, None), P(), P(), P("dp", None, "gz", None, None)),
        out_specs=(P("dp", None, "gz", None, None), P(), P()),
        check_vma=False,
    )
```

profile of v0, /device:TPU:0, one launch (start us, length us, event | category | flops | bytes accessed | tf_op | source)
XLA Modules:
  0.0 216.6 jit_solution(1600772438256316609)
XLA Ops:
  7.2 1.4 copy.8
  8.7 2.4 %collective-permute-start = (bf16[1,32,1,8,128]{4,1,3,2,0:T(8,128)(2,1)S(1)}, bf16[1,32,1,8,128]{4,1,3,2,0:T(8,128)(2,1)S(1)}, u32[]{:S(2)}, u32[]{:S(2)}) collective-permute-start(bf16[1,32,1,8,128]{4,1,3,2,0:T(8,128)(2,1)S(1)} %get-tuple-element.62), channel_id=1, source_target_pairs={{0,16},{1,17},{2,18},{3,19},{4,20},{5,21},{6,22},{7,23},{8,24},{9,... | collective-permute-start | bytes 196616 | tf_op jit(solution)/shard_map/ppermute | solution.py:16
  11.1 1.3 collective-permute-start.1
  12.4 1.1 copy.22
  14.2 0.9 fusion.26
  15.2 0.6 slice_bitcast_fusion.47
  19.9 0.8 fusion.107
  21.1 2.5 %collective-permute-start.2 = (bf16[1,32,1,8,128]{4,1,3,2,0:T(8,128)(2,1)S(1)}, bf16[1,32,1,8,128]{4,1,3,2,0:T(8,128)(2,1)S(1)}, u32[]{:S(2)}, u32[]{:S(2)}) collective-permute-start(bf16[1,32,1,8,128]{4,1,3,2,0:T(8,128)(2,1)S(1)} %get-tuple-element.60), channel_id=1, source_target_pairs={{0,16},{1,17},{2,18},{3,19},{4,20},{5,21},{6,22},{7,23},{8,24},{9,... | collective-permute-start | bytes 196616 | tf_op jit(solution)/shard_map/ppermute | solution.py:16
  23.6 1.5 collective-permute-start.3
  25.1 4.3 %slice_bitcast_fusion.35 = (bf16[3,32,8,8,128]{4,1,0,3,2:T(8,128)(2,1)}, bf16[3,32,8,8,128]{4,1,0,3,2:T(8,128)(2,1)S(1)}, bf16[3,32,8,8,128]{4,1,0,3,2:T(8,128)(...) fusion(bf16[3,1,32,10,10,128]{5,2,0,4,3,1:T(8,128)(2,1)S(1)} %p, ...), kind=kLoop, calls=%fused_computation.72 | loop fusion | bytes 28311552 | tf_op jit(solution)/shard_map/reshape
  29.4 0.9 fusion.24
  30.4 0.6 slice_bitcast_fusion.44
  31.3 3.5 %slice_bitcast_fusion.26 = (bf16[3,32,8,8,128]{4,1,3,2,0:T(8,128)(2,1)S(1)}, bf16[3,32,8,8,128]{4,1,3,2,0:T(8,128)(2,1)S(1)}, bf16[3,32,8,8,128]{4,1,3,2,0:T(8,1...) fusion(bf16[3,1,32,10,10,128]{5,2,4,3,1,0:T(8,128)(2,1)S(1)} %p, ...), kind=kLoop, calls=%fused_computation.63 | loop fusion | bytes 28311552 | tf_op jit(solution)/shard_map/reshape.21
  38.6 0.6 copy-done.7
  39.2 1.3 fusion.137
  40.5 0.5 convolution_bitcast_fusion.12
  45.4 3.0 %collective-permute-start.4 = (bf16[1,32,1,8,128]{4,1,3,2,0:T(8,128)(2,1)S(1)}, bf16[1,32,1,8,128]{4,1,3,2,0:T(8,128)(2,1)S(1)}, u32[]{:S(2)}, u32[]{:S(2)}) collective-permute-start(bf16[1,32,1,8,128]{4,1,3,2,0:T(8,128)(2,1)S(1)} %get-tuple-element.58), channel_id=1, source_target_pairs={{0,16},{1,17},{2,18},{3,19},{4,20},{5,21},{6,22},{7,23},{8,24},{9,... | collective-permute-start | bytes 196616 | tf_op jit(solution)/shard_map/ppermute | solution.py:16
  48.4 1.5 collective-permute-start.5
  50.0 0.8 maximum_bitcast_fusion.1
  50.8 0.8 collective-permute-done.5
  51.6 0.9 fusion.22
  52.5 0.6 slice_bitcast_fusion.41
  53.4 3.5 %slice_bitcast_fusion.17 = (bf16[3,32,8,8,128]{4,1,3,2,0:T(8,128)(2,1)S(1)}, bf16[3,32,8,8,128]{4,1,3,2,0:T(8,128)(2,1)S(1)}, bf16[3,32,8,8,128]{4,1,3,2,0:T(8,1...) fusion(bf16[3,1,32,10,10,128]{5,2,4,3,1,0:T(8,128)(2,1)S(1)} %p, ...), kind=kLoop, calls=%fused_computation.54 | loop fusion | bytes 28311552 | tf_op jit(solution)/shard_map/reshape.39
  60.6 1.3 fusion.136
  62.1 0.5 fusion.108
  62.6 0.8 copy-done.3
  63.4 0.5 fusion.111
  64.1 0.5 fusion.114
  64.7 0.7 copy-done.1
  65.4 0.5 fusion.117
  66.2 0.5 fusion.120
  66.7 0.5 fusion.123
  67.3 0.5 fusion.126
  67.8 0.5 fusion.129
  68.4 0.5 fusion.132
  68.9 2.3 %collective-permute-start.6 = (bf16[1,32,1,8,128]{4,1,3,2,0:T(8,128)(2,1)S(1)}, bf16[1,32,1,8,128]{4,1,3,2,0:T(8,128)(2,1)S(1)}, u32[]{:S(2)}, u32[]{:S(2)}) collective-permute-start(bf16[1,32,1,8,128]{4,1,3,2,0:T(8,128)(2,1)S(1)} %get-tuple-element.56), channel_id=1, source_target_pairs={{0,16},{1,17},{2,18},{3,19},{4,20},{5,21},{6,22},{7,23},{8,24},{9,... | collective-permute-start | bytes 196616 | tf_op jit(solution)/shard_map/ppermute | solution.py:16
  71.2 1.6 collective-permute-start.7
  72.8 0.8 maximum_bitcast_fusion
  73.7 0.7 collective-permute-done.7
  74.4 0.9 select_maximum_fusion
  75.3 0.6 slice_bitcast_fusion.38
  76.2 3.5 %slice_bitcast_fusion.8 = (bf16[3,32,8,8,128]{4,1,3,2,0:T(8,128)(2,1)S(1)}, bf16[3,32,8,8,128]{4,1,3,2,0:T(8,128)(2,1)S(1)}, bf16[3,32,8,8,128]{4,1,3,2,0:T(8,12...) fusion(bf16[3,1,32,10,10,128]{5,2,4,3,1,0:T(8,128)(2,1)S(1)} %p, ...), kind=kLoop, calls=%fused_computation.45 | loop fusion | bytes 28311552 | tf_op jit(solution)/shard_map/reshape.57
  83.5 1.2 fusion.153
  84.6 1.0 copy.78
  85.6 121.0 %all-reduce.7.cloned.1.call-done = (f32[32,32,3,3,3]{0,1,4,3,2:T(8,128)}, f32[32,32,3,3,3]{0,1,4,3,2:T(8,128)}) async-done(((f32[32,32,3,3,3]{0,1,4,3,2:T(8,128)}, f32[32,32,3,3,3]{0,1,4,3,2:T(8,128)}), (f32[32,32,3,3,3]{0,1,4,3,2:T(8,128)}, f32[32,32,3,3,3]{0,1,4,3,2:T(8,128)})) %all-reduce.7.cloned.1.call-update) | async-done | bytes 221200 | tf_op jit(solution)/shard_map/psum | solution.py:92
  206.7 1.1 broadcast_multiply_fusion.1
  207.8 0.9 copy.79
  208.8 0.9 copy.80
  (83 shorter events, 22.0 us)
Async XLA Ops:
  7.2 6.3 %copy-start.5 = (bf16[32,32,3,3,3]{1,0,4,3,2:T(8,128)(2,1)S(1)}, bf16[32,32,3,3,3]{1,0,4,3,2:T(8,128)(2,1)}, u32[]{:S(2)}) copy-start(bf16[32,32,3,3,3]{1,0,4,3,2:T(8,128)(2,1)} %param.5) | copy-start | bytes 165892
  7.2 199.5 %all-reduce.7.cloned.1.call-start = ((), (), s32[]{:S(2)}) async-start(), calls=%async_computation | async-start | bytes 1769472 | tf_op jit(solution)/shard_map/psum | solution.py:92
  8.7 5.0 %collective-permute-start = (bf16[1,32,1,8,128]{4,1,3,2,0:T(8,128)(2,1)S(1)}, bf16[1,32,1,8,128]{4,1,3,2,0:T(8,128)(2,1)S(1)}, u32[]{:S(2)}, u32[]{:S(2)}) collective-permute-start(bf16[1,32,1,8,128]{4,1,3,2,0:T(8,128)(2,1)S(1)} %get-tuple-element.62), channel_id=1, source_target_pairs={{0,16},{1,17},{2,18},{3,19},{4,20},{5,21},{6,22},{7,23},{8,24},{9,... | collective-permute-start | bytes 196616 | tf_op jit(solution)/shard_map/ppermute | solution.py:16
  11.1 3.1 %collective-permute-start.1 = (bf16[1,32,1,8,128]{4,1,3,2,0:T(8,128)(2,1)S(1)}, bf16[1,32,1,8,128]{4,1,3,2,0:T(8,128)(2,1)S(1)}, u32[]{:S(2)}, u32[]{:S(2)}) collective-permute-start(bf16[1,32,1,8,128]{4,1,3,2,0:T(8,128)(2,1)S(1)} %get-tuple-element.63), channel_id=1, source_target_pairs={{16,0},{17,1},{18,2},{19,3},{20,4},{21,5},{22,6},{23,7},{24,8},{25... | collective-permute-start | bytes 196616 | tf_op jit(solution)/shard_map/ppermute | solution.py:17
  21.1 8.4 %collective-permute-start.2 = (bf16[1,32,1,8,128]{4,1,3,2,0:T(8,128)(2,1)S(1)}, bf16[1,32,1,8,128]{4,1,3,2,0:T(8,128)(2,1)S(1)}, u32[]{:S(2)}, u32[]{:S(2)}) collective-permute-start(bf16[1,32,1,8,128]{4,1,3,2,0:T(8,128)(2,1)S(1)} %get-tuple-element.60), channel_id=1, source_target_pairs={{0,16},{1,17},{2,18},{3,19},{4,20},{5,21},{6,22},{7,23},{8,24},{9,... | collective-permute-start | bytes 196616 | tf_op jit(solution)/shard_map/ppermute | solution.py:16
  23.6 5.8 %collective-permute-start.3 = (bf16[1,32,1,8,128]{4,1,3,2,0:T(8,128)(2,1)S(1)}, bf16[1,32,1,8,128]{4,1,3,2,0:T(8,128)(2,1)S(1)}, u32[]{:S(2)}, u32[]{:S(2)}) collective-permute-start(bf16[1,32,1,8,128]{4,1,3,2,0:T(8,128)(2,1)S(1)} %get-tuple-element.61), channel_id=1, source_target_pairs={{16,0},{17,1},{18,2},{19,3},{20,4},{21,5},{22,6},{23,7},{24,8},{25... | collective-permute-start | bytes 196616 | tf_op jit(solution)/shard_map/ppermute | solution.py:17
  31.3 3.6 %copy-start.6 = (bf16[32,32,3,3,3]{1,0,4,3,2:T(8,128)(2,1)S(1)}, bf16[32,32,3,3,3]{1,0,4,3,2:T(8,128)(2,1)}, u32[]{:S(2)}) copy-start(bf16[32,32,3,3,3]{1,0,4,3,2:T(8,128)(2,1)} %param.6) | copy-start | bytes 165892
  38.1 1.0 copy-start.7
  45.4 5.4 %collective-permute-start.4 = (bf16[1,32,1,8,128]{4,1,3,2,0:T(8,128)(2,1)S(1)}, bf16[1,32,1,8,128]{4,1,3,2,0:T(8,128)(2,1)S(1)}, u32[]{:S(2)}, u32[]{:S(2)}) collective-permute-start(bf16[1,32,1,8,128]{4,1,3,2,0:T(8,128)(2,1)S(1)} %get-tuple-element.58), channel_id=1, source_target_pairs={{0,16},{1,17},{2,18},{3,19},{4,20},{5,21},{6,22},{7,23},{8,24},{9,... | collective-permute-start | bytes 196616 | tf_op jit(solution)/shard_map/ppermute | solution.py:16
  48.4 3.1 %collective-permute-start.5 = (bf16[1,32,1,8,128]{4,1,3,2,0:T(8,128)(2,1)S(1)}, bf16[1,32,1,8,128]{4,1,3,2,0:T(8,128)(2,1)S(1)}, u32[]{:S(2)}, u32[]{:S(2)}) collective-permute-start(bf16[1,32,1,8,128]{4,1,3,2,0:T(8,128)(2,1)S(1)} %get-tuple-element.59), channel_id=1, source_target_pairs={{16,0},{17,1},{18,2},{19,3},{20,4},{21,5},{22,6},{23,7},{24,8},{25... | collective-permute-start | bytes 196616 | tf_op jit(solution)/shard_map/ppermute | solution.py:17
  60.6 1.4 copy-start.4
  62.0 1.4 copy-start.3
  62.6 1.5 copy-start.2
  63.9 1.5 copy-start.1
  64.7 1.5 copy-start
  68.9 4.7 %collective-permute-start.6 = (bf16[1,32,1,8,128]{4,1,3,2,0:T(8,128)(2,1)S(1)}, bf16[1,32,1,8,128]{4,1,3,2,0:T(8,128)(2,1)S(1)}, u32[]{:S(2)}, u32[]{:S(2)}) collective-permute-start(bf16[1,32,1,8,128]{4,1,3,2,0:T(8,128)(2,1)S(1)} %get-tuple-element.56), channel_id=1, source_target_pairs={{0,16},{1,17},{2,18},{3,19},{4,20},{5,21},{6,22},{7,23},{8,24},{9,... | collective-permute-start | bytes 196616 | tf_op jit(solution)/shard_map/ppermute | solution.py:16
  71.2 3.1 %collective-permute-start.7 = (bf16[1,32,1,8,128]{4,1,3,2,0:T(8,128)(2,1)S(1)}, bf16[1,32,1,8,128]{4,1,3,2,0:T(8,128)(2,1)S(1)}, u32[]{:S(2)}, u32[]{:S(2)}) collective-permute-start(bf16[1,32,1,8,128]{4,1,3,2,0:T(8,128)(2,1)S(1)} %get-tuple-element.57), channel_id=1, source_target_pairs={{16,0},{17,1},{18,2},{19,3},{20,4},{21,5},{22,6},{23,7},{24,8},{25... | collective-permute-start | bytes 196616 | tf_op jit(solution)/shard_map/ppermute | solution.py:17
  206.7 2.1 copy-start.8
Sparse Core Ops, SparseCore 0:
  73.8 132.8 all-reduce.6
where the time goes:
time: 217 us
  waiting for transfers between devices  123 us (57%)
  local copies, waits for them, and re-layouts  25.8 us (12%)
  matrix products  25.3 us (12%)
  starting transfers between devices  16.1 us (7%)
  between operations  14.6 us (7%)
  other arithmetic  11.7 us (5%)
    psum x1, waiting for transfers between devices, local(): total_one, total_two = lax.psum((term_one, term_two), ('gz', 'dp'))  121 us
    dot_general x36, matrix products, convolve_valid(): jnp.einsum('oki,kizyx->ozyx', weights, window, preferred_element_type=jnp...  15.7 us
    another operation x3, local copies, waits for them, and re-layouts  10.6 us
    ppermute x4, starting transfers between devices, extended(): before = lax.ppermute(last, axis, up)  10.2 us
    dot_general x18, matrix products, kernel_terms(): jnp.einsum('ozyx,kizyx->oik', grad, window, preferred_element_type=jnp.fl...  9.6 us
    unnamed x24, local copies, waits for them, and re-layouts  8.24 us
    ppermute x4, starting transfers between devices, extended(): after = lax.ppermute(initial, axis, down)  5.83 us
  transfers between devices with their start and end apart: 9, of which 4 were waited for; matrix products, arithmetic and copies ran while one was open for 9% of the time, Pallas kernels for 0%

commit v1 on v0

v1 whole, which is shorter than its diff:
```python
import functools
import math

import jax
import jax.numpy as jnp
from jax import lax
from jax.experimental import pallas as pl
from jax.experimental.pallas import tpu as pltpu
from jax.sharding import PartitionSpec as P

MESH = pl.DeviceIdType.MESH
F32 = jnp.float32
BF16 = jnp.bfloat16
TAPS = [(plane, col) for plane in range(3) for col in range(3)]
NN = (((1,), (0,)), ((), ()))
NT = (((1,), (1,)), ((), ()))


def dot(a, b, dims=NN):
    return lax.dot_general(a, b, dims, preferred_element_type=F32)


def iota(shape, dim):
    return lax.broadcasted_iota(jnp.int32, shape, dim)


def one_hot(mask):
    return jnp.where(mask, 1.0, 0.0).astype(BF16)


def sigmoid(v):
    return 0.5 * jnp.tanh(0.5 * v) + 0.5


def kernel(
    sizes,
    factor,
    x_ref,
    w1_ref,
    w2_ref,
    cot_ref,
    out_ref,
    g1_ref,
    g2_ref,
    s_in,
    s_hid,
    s_g2,
    s_g1,
    wcat,
    slope,
    bands,
    packed,
    arrived,
    full,
    halo_send,
    halo_recv,
    rs_send,
    rs_recv,
    ag_send,
    ag_recv,
):
    gz_count, dp_count, owners = sizes
    chan, depth, height, width = x_ref.shape
    rows = chan * height
    count = gz_count * dp_count
    gz = lax.axis_index("gz")
    dp = lax.axis_index("dp")
    me = gz * dp_count + dp

    def place(dev):
        return {"gz": dev // dp_count, "dp": lax.rem(dev, dp_count)}

    barrier = pltpu.get_barrier_semaphore()

    def greet(k, carry):
        dev = lax.rem(me + k, count)
        pl.semaphore_signal(barrier, inc=1, device_id=place(dev), device_id_type=MESH)
        return carry

    lax.fori_loop(1, count, greet, 0)

    r, l = iota((rows, rows), 0), iota((rows, rows), 1)
    to_rows = one_hot((r // chan == l % height) & (r % chan == l // height))
    to_chan = one_hot((r // height == l % chan) & (r % height == l // chan))

    def shifts(s, p, value):
        lane = iota(value.shape, 1)
        s[0, p] = jnp.where(lane == 0, 0.0, pltpu.roll(value, 1, 1)).astype(BF16)
        s[2, p] = jnp.where(lane == width - 1, 0.0, pltpu.roll(value, width - 1, 1)).astype(BF16)

    def put(s, p, value):
        s[1, p] = value.astype(BF16)
        shifts(s, p, value)

    def up_copy(n, s):
        return pltpu.make_async_remote_copy(
            src_ref=s.at[1, depth],
            dst_ref=s.at[1, 0],
            send_sem=halo_send.at[n, 0],
            recv_sem=halo_recv.at[n, 0],
            device_id={"gz": gz + 1, "dp": dp},
            device_id_type=MESH,
        )

    def down_copy(n, s):
        return pltpu.make_async_remote_copy(
            src_ref=s.at[1, 1],
            dst_ref=s.at[1, depth + 1],
            send_sem=halo_send.at[n, 1],
            recv_sem=halo_recv.at[n, 1],
            device_id={"gz": gz - 1, "dp": dp},
            device_id_type=MESH,
        )

    def send_halo(n, s):
        @pl.when(gz < gz_count - 1)
        def _():
            up_copy(n, s).start()

        @pl.when(gz > 0)
        def _():
            down_copy(n, s).start()

    def take_halo(n, s):
        @pl.when(gz > 0)
        def _():
            up_copy(n, s).wait_recv()

        @pl.when(gz == 0)
        def _():
            s[1, 0] = jnp.zeros((rows, width), BF16)

        @pl.when(gz < gz_count - 1)
        def _():
            down_copy(n, s).wait_recv()

        @pl.when(gz == gz_count - 1)
        def _():
            s[1, depth + 1] = jnp.zeros((rows, width), BF16)

        for p in (0, depth + 1):
            shifts(s, p, s[1, p].astype(F32))

    def raw(ref, p):
        return ref[:, p].astype(F32).reshape(rows, width).astype(BF16)

    edges = sorted({0, depth - 1})
    inner = [p for p in range(depth) if p not in edges]
    groups = [edges] + [inner[i : i + 2] for i in range(0, len(inner), 2)]

    def lanes(parts):
        return parts[0] if len(parts) == 1 else jnp.concatenate(parts, axis=1)

    def load(ref, planes):
        value = dot(to_rows, lanes([raw(ref, p) for p in planes]))
        return [value[:, i * width : (i + 1) * width] for i in range(len(planes))]

    def conv(n, s, planes):
        window = jnp.concatenate(
            [lanes([s[col, p + plane] for p in planes]) for plane, col in TAPS], axis=0
        )
        value = dot(wcat[n], window)
        return [value[:, i * width : (i + 1) * width] for i in range(len(planes))]

    for planes in groups:
        for p, value in zip(planes, load(x_ref, planes)):
            put(s_in, p + 1, value)

    pack = 4 * chan
    er, el = iota((chan, pack), 0), iota((chan, pack), 1)
    spots = [one_hot(el == er + off * chan) for off in range(3)]
    eye = one_hot(iota((chan, chan), 0) == iota((chan, chan), 1))
    pieces = []
    for ref in (w1_ref, w2_ref):
        base = None
        for off in range(3):
            tall = jnp.concatenate([ref[9 * a + 3 * off + b] for a, b in TAPS], axis=0)
            piece = dot(tall, spots[off])
            base = piece if base is None else base + piece
        pieces.append(base.astype(BF16))
    blank = jnp.zeros((chan, chan), BF16)
    for ref in (w2_ref, w1_ref):
        for a, b in TAPS:
            tall = jnp.concatenate(
                [ref[26 - (9 * a + 3 * off + b)] for off in range(3)] + [blank], axis=0
            )
            pieces.append(dot(eye, tall, NT).astype(BF16))
    base = jnp.concatenate(pieces, axis=0)
    sr, sl = iota((pack, rows), 0), iota((pack, rows), 1)
    for y in range(height):
        pick = one_hot(
            (sr % chan == sl % chan)
            & (sl // chan == y - 1 + sr // chan)
            & (sr < 3 * chan)
        )
        placed = dot(base, pick).astype(BF16)
        for n in range(4):
            for t in range(9):
                at = (n * 9 + t) * chan
                wcat[n, y * chan : (y + 1) * chan, t * rows : (t + 1) * rows] = placed[
                    at : at + chan
                ]

    pl.semaphore_wait(barrier, count - 1)
    send_halo(0, s_in)

    def scatter_terms(j):
        def step(k, carry):
            dev = lax.rem(me + k, count)

            @pl.when(dev < owners)
            def _():
                pltpu.make_async_remote_copy(
                    src_ref=packed.at[j, dev],
                    dst_ref=arrived.at[j, count - 1 - k],
                    send_sem=rs_send.at[j],
                    recv_sem=rs_recv.at[j],
                    device_id=place(dev),
                    device_id_type=MESH,
                ).start()

            return carry

        lax.fori_loop(1, count, step, 0)

    def wait_for(ref, sem):
        pltpu.make_async_copy(ref, ref, sem).wait()

    def gather_terms(j):
        @pl.when(me < owners)
        def _():
            wait_for(arrived.at[j], rs_recv.at[j])
            full[j, me] = (jnp.sum(arrived[j], axis=0) + packed[j, me]) * factor

            def step(k, carry):
                dev = lax.rem(me + k, count)
                pltpu.make_async_remote_copy(
                    src_ref=full.at[j, me],
                    dst_ref=full.at[j, me],
                    send_sem=ag_send.at[j],
                    recv_sem=ag_recv.at[j],
                    device_id=place(dev),
                    device_id_type=MESH,
                ).start()
                return carry

            lax.fori_loop(1, count, step, 0)

    def finish_terms(j, ref):
        @pl.when(me < owners)
        def _():
            wait_for(full.at[j, pl.ds(0, owners - 1)], ag_recv.at[j])
            wait_for(packed.at[j, pl.ds(0, owners - 1)], rs_send.at[j])
            wait_for(arrived.at[j], ag_send.at[j])

        @pl.when(me >= owners)
        def _():
            wait_for(full.at[j, pl.ds(0, owners)], ag_recv.at[j])
            wait_for(packed.at[j, pl.ds(0, owners)], rs_send.at[j])

        tiles = full.shape[2]
        value = full[j].reshape(owners * tiles, 8, 128)
        for g in range(4):
            ref[:, g * 8 : (g + 1) * 8, :] = value[:27, :, g * chan : (g + 1) * chan]

    qr, ql = iota((4 * rows, 128), 0), iota((4 * rows, 128), 1)
    gather_rows = one_hot((qr // rows == ql // chan) & (qr % chan == ql % chan))

    def terms(j, s, s_grad):
        grad = lanes([s_grad[1, p + 1] for p in range(depth)])
        block = iota((chan, rows), 1) // chan
        for plane, col in TAPS:
            window = lanes([s[col, p + plane] for p in range(depth)])
            value = dot(grad, window, NT)
            for off in range(3):
                band = jnp.zeros((chan, rows), F32)
                for y in range(height):
                    if 0 <= y + off - 1 < height:
                        part = value[y * chan : (y + 1) * chan]
                        band = jnp.where(block == y + off - 1, part, band)
                t = plane * 9 + off * 3 + col
                for g in range(4):
                    bands[t * 8 : (t + 1) * 8, g * rows : (g + 1) * rows] = band[
                        g * 8 : (g + 1) * 8
                    ]
        value = bands[...]
        high = value.astype(BF16)
        low = (value - high.astype(F32)).astype(BF16)
        total = (dot(high, gather_rows) + dot(low, gather_rows)).reshape(27, 8, 128)
        tiles = packed.shape[2]
        for t in range(27):
            packed[j, t // tiles, t % tiles] = total[t]

    if owners * packed.shape[2] > 27:
        packed[...] = jnp.zeros_like(packed)

    take_halo(0, s_in)
    for i, planes in enumerate(groups):
        for p, pre in zip(planes, conv(0, s_in, planes)):
            sig = sigmoid(pre)
            slope[p] = sig * (1.0 + pre * (1.0 - sig))
            put(s_hid, p + 1, pre * sig)
        if i == 0:
            send_halo(1, s_hid)
    take_halo(1, s_hid)
    for i, planes in enumerate(groups):
        for p, pre, cot in zip(planes, conv(1, s_hid, planes), load(cot_ref, planes)):
            sig = sigmoid(pre)
            put(s_g2, p + 1, cot * (sig * (1.0 + pre * (1.0 - sig))))
        if i == 0:
            send_halo(2, s_g2)
    terms(1, s_hid, s_g2)
    scatter_terms(1)
    take_halo(2, s_g2)
    for i, planes in enumerate(groups):
        for p, value in zip(planes, conv(2, s_g2, planes)):
            put(s_g1, p + 1, value * slope[p])
        if i == 0:
            send_halo(3, s_g1)
    gather_terms(1)
    terms(0, s_in, s_g1)
    scatter_terms(0)
    take_halo(3, s_g1)
    for planes in groups:
        value = lanes([v.astype(BF16) for v in conv(3, s_g1, planes)])
        value = dot(to_chan, value)
        for i, p in enumerate(planes):
            part = value[:, i * width : (i + 1) * width]
            out_ref[:, p] = part.reshape(chan, height, width).astype(BF16)
    gather_terms(0)
    finish_terms(1, g2_ref)
    finish_terms(0, g1_ref)

    for n, s in enumerate((s_in, s_hid, s_g2, s_g1)):

        @pl.when(gz < gz_count - 1)
        def _():
            up_copy(n, s).wait_send()

        @pl.when(gz > 0)
        def _():
            down_copy(n, s).wait_send()


def solution(mesh):
    gz_count, dp_count = mesh.shape["gz"], mesh.shape["dp"]
    count = gz_count * dp_count

    def local(inputs, kernel_one, kernel_two, cotangent):
        _, chan, depth, height, width = inputs.shape
        rows = chan * height
        cells = dp_count * gz_count * depth * height * width
        tiles = -(-27 // count)
        owners = -(-27 // tiles)
        taps = lambda k: k.transpose(2, 3, 4, 0, 1).reshape(27, chan, chan)
        slab = pltpu.VMEM((3, depth + 2, rows, width), BF16)
        vmem = pl.BlockSpec(memory_space=pltpu.VMEM)
        out, g1, g2 = pl.pallas_call(
            functools.partial(kernel, (gz_count, dp_count, owners), 1.0 / math.sqrt(cells)),
            out_shape=(
                jax.ShapeDtypeStruct((chan, depth, height, width), BF16),
                jax.ShapeDtypeStruct((27, chan, chan), F32),
                jax.ShapeDtypeStruct((27, chan, chan), F32),
            ),
            in_specs=[vmem] * 4,
            out_specs=(vmem, vmem, vmem),
            scratch_shapes=[
                slab,
                slab,
                slab,
                slab,
                pltpu.VMEM((4, rows, 9 * rows), BF16),
                pltpu.VMEM((depth, rows, width), F32),
                pltpu.VMEM((27 * 8, 4 * rows), F32),
                pltpu.VMEM((2, owners, tiles, 8, 128), F32),
                pltpu.VMEM((2, count - 1, tiles, 8, 128), F32),
                pltpu.VMEM((2, owners, tiles, 8, 128), F32),
                pltpu.SemaphoreType.DMA((4, 2)),
                pltpu.SemaphoreType.DMA((4, 2)),
                pltpu.SemaphoreType.DMA((2,)),
                pltpu.SemaphoreType.DMA((2,)),
                pltpu.SemaphoreType.DMA((2,)),
                pltpu.SemaphoreType.DMA((2,)),
            ],
            compiler_params=pltpu.CompilerParams(collective_id=0, has_side_effects=True),
        )(inputs[0], taps(kernel_one), taps(kernel_two), cotangent[0])
        back = lambda g: g.reshape(3, 3, 3, chan, chan).transpose(3, 4, 0, 1, 2)
        return out[None], back(g1), back(g2)

    return jax.shard_map(
        local,
        mesh=mesh,
        in_specs=(P("dp", None, "gz", None, None), P(), P(), P("dp", None, "gz", None, None)),
        out_specs=(P("dp", None, "gz", None, None), P(), P()),
        check_vma=False,
    )
```

time: 217 us -> 39.5 us (0.18)
  waiting for transfers between devices: 123 us -> 0 us
  Pallas kernels: 0 us -> 34.8 us
  matrix products: 25.3 us -> 0 us
  local copies, waits for them, and re-layouts: 25.8 us -> 3.86 us
  starting transfers between devices: 16.1 us -> 0 us
  between operations: 14.6 us -> 0.65 us
  other arithmetic: 11.7 us -> 0 us
    psum x1 -> x0, waiting for transfers between devices: 121 us -> none  [local(): total_one, total_two = lax.psum((term_one, term_two), ('gz', 'dp'))]
    pallas_call x0 -> x1, Pallas kernels: none -> 34.8 us  [local(): pl.pallas_call(functools.partial(kernel, (gz_count, dp_count, owners), 1....]
    dot_general x54 -> x0, matrix products: 25.3 us -> none  [the longest x36 15.7 us: convolve_valid(): jnp.einsum('oki,kizyx->ozyx', weights, window, preferred_element_type=jnp...]
    ppermute x8 -> x0, starting transfers between devices: 16 us -> none  [the longest x4 10.2 us: extended(): before = lax.ppermute(last, axis, up)]
    another operation x7 -> x0, local copies, waits for them, and re-layouts: 13.1 us -> none
    unnamed x24 -> x7, local copies, waits for them, and re-layouts: 8.24 us -> 3.86 us
    reshape x1 -> x0, local copies, waits for them, and re-layouts: 4.33 us -> none
    convert_element_type x4 -> x0, other arithmetic: 4.09 us -> none  [the longest x1 1.33 us: local(): (cotangent.astype(jnp.float32) * dsilu(pre_two)).astype(jnp.bfloat16)]
  transfers between devices with their start and end apart: 9 -> 0, of which waited for: 4 -> 0; matrix products, arithmetic and copies ran while one was open for 9% -> 0% of each run, Pallas kernels for 0% -> 0%
where the time goes in v1:
time: 39.5 us; the launch traced here: 39.3 us
  Pallas kernels  34.8 us (88%)
  local copies, waits for them, and re-layouts  3.86 us (10%)
  between operations  0.65 us (2%)
    pallas_call x1, Pallas kernels, local(): pl.pallas_call(functools.partial(kernel, (gz_count, dp_count, owners), 1....  34.8 us
    unnamed x7, local copies, waits for them, and re-layouts  3.86 us

profile of v1, /device:TPU:0, one launch (start us, length us, event | category | flops | bytes accessed | tf_op | source)
XLA Modules:
  0.0 39.3 jit_solution(17935152699050136518)
XLA Ops:
  0.6 34.8 %shard_map.67 = (bf16[32,8,8,128]{3,2,1,0:T(8,128)(2,1)}, f32[27,32,32]{2,1,0:T(8,128)}, f32[27,32,32]{2,1,0:T(8,128)}) custom-call(bf16[32,8,8,128]{3,2,1,0:T(8,128)(2,1)} %bitcast.15, bf16[27,32,32]{2,1,0:T(8,128)(2,1)} %bitcast.20, bf16[27,32,32]{2,1,0:T(8,128)(2,1)} %bitcast.21, bf16[32,8,8,128]{3,2,1,0:T(8,128)(2,1)} %bitcast.16), custom_call_target="tpu_custom_call" | custom-call | tf_op jit(solution)/shard_map/pallas_call | solution.py:358
  35.5 0.0 copy-start.1
  35.5 1.9 %copy.10 = bf16[1,32,8,8,128]{4,3,2,1,0:T(8,128)(2,1)} copy(bf16[1,32,8,8,128]{4,3,2,1,0:T(8,128)(2,1)} %bitcast.17) | data formatting | bytes 1048576
  37.4 0.0 copy-done.1
  37.4 0.0 copy-start
  37.4 0.8 %copy.11 = f32[32,32,3,3,3]{1,0,4,3,2:T(8,128)} copy(f32[32,32,3,3,3]{1,0,4,3,2:T(8,128)S(1)} %bitcast.19) | data formatting | bytes 221184
  38.2 0.4 %copy-done = f32[27,32,32]{2,1,0:T(8,128)S(1)} copy-done((f32[27,32,32]{2,1,0:T(8,128)S(1)}, f32[27,32,32]{2,1,0:T(8,128)}, u32[]{:S(2)}) %copy-start) | copy-done | bytes 110616
  38.6 0.8 %copy.12 = f32[32,32,3,3,3]{1,0,4,3,2:T(8,128)} copy(f32[32,32,3,3,3]{1,0,4,3,2:T(8,128)S(1)} %bitcast.18) | data formatting | bytes 221184
Async XLA Ops:
  35.5 1.9 %copy-start.1 = (f32[27,32,32]{2,1,0:T(8,128)S(1)}, f32[27,32,32]{2,1,0:T(8,128)}, u32[]{:S(2)}) copy-start(f32[27,32,32]{2,1,0:T(8,128)} %get-tuple-element.7) | copy-start | bytes 331780
  37.4 1.2 %copy-start = (f32[27,32,32]{2,1,0:T(8,128)S(1)}, f32[27,32,32]{2,1,0:T(8,128)}, u32[]{:S(2)}) copy-start(f32[27,32,32]{2,1,0:T(8,128)} %get-tuple-element.8) | copy-start | bytes 331780

commit v2 on v1

--- a/solution.py
+++ b/solution.py
@@ -35,13 +35,16 @@
 def kernel(
     sizes,
     factor,
+    x_hbm,
+    w1_hbm,
+    w2_hbm,
+    cot_hbm,
+    res_ref,
+    sums_ref,
     x_ref,
     w1_ref,
     w2_ref,
     cot_ref,
-    out_ref,
-    g1_ref,
-    g2_ref,
     s_in,
     s_hid,
     s_g2,
@@ -58,6 +61,7 @@
     rs_recv,
     ag_send,
     ag_recv,
+    load_sem,
 ):
     gz_count, dp_count, owners = sizes
     chan, depth, height, width = x_ref.shape
@@ -70,6 +74,15 @@
     def place(dev):
         return {"gz": dev // dp_count, "dp": lax.rem(dev, dp_count)}
 
+    loads = [
+        pltpu.make_async_copy(src, dst, load_sem.at[i])
+        for i, (src, dst) in enumerate(
+            ((w1_hbm, w1_ref), (x_hbm, x_ref), (w2_hbm, w2_ref), (cot_hbm, cot_ref))
+        )
+    ]
+    for copy in loads:
+        copy.start()
+
     barrier = pltpu.get_barrier_semaphore()
 
     def greet(k, carry):
@@ -81,7 +94,6 @@
 
     r, l = iota((rows, rows), 0), iota((rows, rows), 1)
     to_rows = one_hot((r // chan == l % height) & (r % chan == l // height))
-    to_chan = one_hot((r // height == l % chan) & (r % height == l // chan))
 
     def shifts(s, p, value):
         lane = iota(value.shape, 1)
@@ -162,47 +174,43 @@
         value = dot(wcat[n], window)
         return [value[:, i * width : (i + 1) * width] for i in range(len(planes))]
 
-    for planes in groups:
-        for p, value in zip(planes, load(x_ref, planes)):
-            put(s_in, p + 1, value)
-
     pack = 4 * chan
     er, el = iota((chan, pack), 0), iota((chan, pack), 1)
-    spots = [one_hot(el == er + off * chan) for off in range(3)]
     eye = one_hot(iota((chan, chan), 0) == iota((chan, chan), 1))
-    pieces = []
-    for ref in (w1_ref, w2_ref):
+    blank = jnp.zeros((chan, chan), BF16)
+    sr, sl = iota((pack, rows), 0), iota((pack, rows), 1)
+
+    def forward(ref):
         base = None
         for off in range(3):
             tall = jnp.concatenate([ref[9 * a + 3 * off + b] for a, b in TAPS], axis=0)
-            piece = dot(tall, spots[off])
+            piece = dot(tall, one_hot(el == er + off * chan))
             base = piece if base is None else base + piece
-        pieces.append(base.astype(BF16))
-    blank = jnp.zeros((chan, chan), BF16)
-    for ref in (w2_ref, w1_ref):
+        return [base.astype(BF16)]
+
+    def backward(ref):
+        pieces = []
         for a, b in TAPS:
             tall = jnp.concatenate(
                 [ref[26 - (9 * a + 3 * off + b)] for off in range(3)] + [blank], axis=0
             )
             pieces.append(dot(eye, tall, NT).astype(BF16))
-    base = jnp.concatenate(pieces, axis=0)
-    sr, sl = iota((pack, rows), 0), iota((pack, rows), 1)
-    for y in range(height):
-        pick = one_hot(
-            (sr % chan == sl % chan)
-            & (sl // chan == y - 1 + sr // chan)
-            & (sr < 3 * chan)
-        )
-        placed = dot(base, pick).astype(BF16)
-        for n in range(4):
-            for t in range(9):
-                at = (n * 9 + t) * chan
+        return pieces
+
+    def spread(first, pieces):
+        base = jnp.concatenate(pieces, axis=0)
+        for y in range(height):
+            pick = one_hot(
+                (sr % chan == sl % chan)
+                & (sl // chan == y - 1 + sr // chan)
+                & (sr < 3 * chan)
+            )
+            placed = dot(base, pick).astype(BF16)
+            for at in range(base.shape[0] // chan):
+                n, t = first + at // 9, at % 9
                 wcat[n, y * chan : (y + 1) * chan, t * rows : (t + 1) * rows] = placed[
-                    at : at + chan
+                    at * chan : (at + 1) * chan
                 ]
-
-    pl.semaphore_wait(barrier, count - 1)
-    send_halo(0, s_in)
 
     def scatter_terms(j):
         def step(k, carry):
@@ -246,7 +254,7 @@
 
             lax.fori_loop(1, count, step, 0)
 
-    def finish_terms(j, ref):
+    def finish_terms(j):
         @pl.when(me < owners)
         def _():
             wait_for(full.at[j, pl.ds(0, owners - 1)], ag_recv.at[j])
@@ -258,10 +266,7 @@
             wait_for(full.at[j, pl.ds(0, owners)], ag_recv.at[j])
             wait_for(packed.at[j, pl.ds(0, owners)], rs_send.at[j])
 
-        tiles = full.shape[2]
-        value = full[j].reshape(owners * tiles, 8, 128)
-        for g in range(4):
-            ref[:, g * 8 : (g + 1) * 8, :] = value[:27, :, g * chan : (g + 1) * chan]
+        sums_ref[j] = full[j].reshape(owners * full.shape[2], 8, 128)[:27]
 
     qr, ql = iota((4 * rows, 128), 0), iota((4 * rows, 128), 1)
     gather_rows = one_hot((qr // rows == ql // chan) & (qr % chan == ql % chan))
@@ -294,52 +299,86 @@
     if owners * packed.shape[2] > 27:
         packed[...] = jnp.zeros_like(packed)
 
-    take_halo(0, s_in)
-    for i, planes in enumerate(groups):
+    def first_layer(planes):
         for p, pre in zip(planes, conv(0, s_in, planes)):
             sig = sigmoid(pre)
             slope[p] = sig * (1.0 + pre * (1.0 - sig))
             put(s_hid, p + 1, pre * sig)
-        if i == 0:
-            send_halo(1, s_hid)
-    take_halo(1, s_hid)
-    for i, planes in enumerate(groups):
+
+    def second_layer(planes):
         for p, pre, cot in zip(planes, conv(1, s_hid, planes), load(cot_ref, planes)):
             sig = sigmoid(pre)
             put(s_g2, p + 1, cot * (sig * (1.0 + pre * (1.0 - sig))))
-        if i == 0:
-            send_halo(2, s_g2)
+
+    def second_back(planes):
+        for p, value in zip(planes, conv(2, s_g2, planes)):
+            put(s_g1, p + 1, value * slope[p])
+
+    loads[0].wait()
+    spread(0, forward(w1_ref))
+    loads[1].wait()
+    for planes in groups:
+        for p, value in zip(planes, load(x_ref, planes)):
+            put(s_in, p + 1, value)
+    for planes in groups[1:]:
+        first_layer(planes)
+    pl.semaphore_wait(barrier, count - 1)
+    send_halo(0, s_in)
+    for copy in loads[2:]:
+        copy.wait()
+    spread(1, forward(w2_ref))
+    take_halo(0, s_in)
+    first_layer(groups[0])
+    send_halo(1, s_hid)
+    for planes in groups[1:]:
+        second_layer(planes)
+    spread(2, backward(w2_ref) + backward(w1_ref))
+    take_halo(1, s_hid)
+    second_layer(groups[0])
+    send_halo(2, s_g2)
     terms(1, s_hid, s_g2)
     scatter_terms(1)
     take_halo(2, s_g2)
     for i, planes in enumerate(groups):
-        for p, value in zip(planes, conv(2, s_g2, planes)):
-            put(s_g1, p + 1, value * slope[p])
+        second_back(planes)
         if i == 0:
             send_halo(3, s_g1)
-    gather_terms(1)
     terms(0, s_in, s_g1)
     scatter_terms(0)
+    gather_terms(1)
     take_halo(3, s_g1)
     for planes in groups:
-        value = lanes([v.astype(BF16) for v in conv(3, s_g1, planes)])
-        value = dot(to_chan, value)
+        for p, value in zip(planes, conv(3, s_g1, planes)):
+            res_ref[p] = value.astype(BF16)
+    gather_terms(0)
+    finish_terms(1)
+    finish_terms(0)
+
+    for n, s in enumerate((s_in, s_hid, s_g2, s_g1)):
+
+        @pl.when(gz < gz_count - 1)
+        def _():
+            up_copy(n, s).wait_send()
+
+        @pl.when(gz > 0)
+        def _():
+            down_copy(n, s).wait_send()
+
+
+def unpack(res_ref, sums_ref, out_ref, g1_ref, g2_ref):
+    chan, depth, height, width = out_ref.shape
+    rows = chan * height
+    for j, ref in enumerate((g1_ref, g2_ref)):
+        for g in range(4):
+            ref[:, g * 8 : (g + 1) * 8, :] = sums_ref[j, :, :, g * chan : (g + 1) * chan]
+    r, l = iota((rows, rows), 0), iota((rows, rows), 1)
+    to_chan = one_hot((r // height == l % chan) & (r % height == l // chan))
+    for at in range(0, depth, 2):
+        planes = range(at, min(at + 2, depth))
+        value = dot(to_chan, jnp.concatenate([res_ref[p] for p in planes], axis=1))
         for i, p in enumerate(planes):
             part = value[:, i * width : (i + 1) * width]
             out_ref[:, p] = part.reshape(chan, height, width).astype(BF16)
-    gather_terms(0)
-    finish_terms(1, g2_ref)
-    finish_terms(0, g1_ref)
-
-    for n, s in enumerate((s_in, s_hid, s_g2, s_g1)):
-
-        @pl.when(gz < gz_count - 1)
-        def _():
-            up_copy(n, s).wait_send()
-
-        @pl.when(gz > 0)
-        def _():
-            down_copy(n, s).wait_send()
 
 
 def solution(mesh):
@@ -355,16 +394,19 @@
         taps = lambda k: k.transpose(2, 3, 4, 0, 1).reshape(27, chan, chan)
         slab = pltpu.VMEM((3, depth + 2, rows, width), BF16)
         vmem = pl.BlockSpec(memory_space=pltpu.VMEM)
-        out, g1, g2 = pl.pallas_call(
+        res, sums = pl.pallas_call(
             functools.partial(kernel, (gz_count, dp_count, owners), 1.0 / math.sqrt(cells)),
             out_shape=(
-                jax.ShapeDtypeStruct((chan, depth, height, width), BF16),
-                jax.ShapeDtypeStruct((27, chan, chan), F32),
-                jax.ShapeDtypeStruct((27, chan, chan), F32),
+                jax.ShapeDtypeStruct((depth, rows, width), BF16),
+                jax.ShapeDtypeStruct((2, 27, 8, 128), F32),
             ),
-            in_specs=[vmem] * 4,
-            out_specs=(vmem, vmem, vmem),
+            in_specs=[pl.BlockSpec(memory_space=pl.ANY)] * 4,
+            out_specs=(vmem, vmem),
             scratch_shapes=[
+                pltpu.VMEM((chan, depth, height, width), BF16),
+                pltpu.VMEM((27, chan, chan), BF16),
+                pltpu.VMEM((27, chan, chan), BF16),
+                pltpu.VMEM((chan, depth, height, width), BF16),
                 slab,
                 slab,
                 slab,
@@ -381,9 +423,20 @@
                 pltpu.SemaphoreType.DMA((2,)),
                 pltpu.SemaphoreType.DMA((2,)),
                 pltpu.SemaphoreType.DMA((2,)),
+                pltpu.SemaphoreType.DMA((4,)),
             ],
             compiler_params=pltpu.CompilerParams(collective_id=0, has_side_effects=True),
         )(inputs[0], taps(kernel_one), taps(kernel_two), cotangent[0])
+        out, g1, g2 = pl.pallas_call(
+            unpack,
+            out_shape=(
+                jax.ShapeDtypeStruct((chan, depth, height, width), BF16),
+                jax.ShapeDtypeStruct((27, chan, chan), F32),
+                jax.ShapeDtypeStruct((27, chan, chan), F32),
+            ),
+            in_specs=[vmem] * 2,
+            out_specs=(vmem, vmem, vmem),
+        )(res, sums)
         back = lambda g: g.reshape(3, 3, 3, chan, chan).transpose(3, 4, 0, 1, 2)
         return out[None], back(g1), back(g2)
 

time: 39.5 us -> 34.1 us (0.86)
  local copies, waits for them, and re-layouts: 3.86 us -> 0 us
  Pallas kernels: 34.8 us -> 33.3 us
    pallas_call x1, Pallas kernels: 34.8 us -> 30.9 us  [local(): pl.pallas_call(functools.partial(kernel, (gz_count, dp_count, owners), 1....]
    unnamed x7 -> x0, local copies, waits for them, and re-layouts: 3.86 us -> none
    pallas_call x0 -> x1, Pallas kernels: none -> 2.43 us  [local(): pl.pallas_call(unpack, out_shape=(jax.ShapeDtypeStruct((chan, depth, heig...]
where the time goes in v2:
time: 34.1 us; the launch traced here: 34 us
  Pallas kernels  33.3 us (98%)
  between operations  0.64 us (2%)
    pallas_call x1, Pallas kernels, local(): pl.pallas_call(functools.partial(kernel, (gz_count, dp_count, owners), 1....  30.9 us
    pallas_call x1, Pallas kernels, local(): pl.pallas_call(unpack, out_shape=(jax.ShapeDtypeStruct((chan, depth, heig...  2.43 us

profile of v2, /device:TPU:0, one launch (start us, length us, event | category | flops | bytes accessed | tf_op | source)
XLA Modules:
  0.0 34.0 jit_solution(14896252799005774530)
XLA Ops:
  0.6 30.9 %shard_map.67 = (bf16[8,256,128]{2,1,0:T(8,128)(2,1)}, f32[2,27,8,128]{3,2,1,0:T(8,128)}) custom-call(bf16[32,8,8,128]{3,2,1,0:T(8,128)(2,1)} %bitcast.15, bf16[27,32,32]{2,1,0:T(8,128)(2,1)} %bitcast.17, bf16[27,32,32]{2,1,0:T(8,128)(2,1)} %bitcast.18, bf16[32,8,8,128]{3,2,1,0:T(8,128)(2,1)} %bitcast.16), custom_call_target="tpu_custom_call" | custom-call | tf_op jit(solution)/shard_map/pallas_call | solution.py:397
  31.5 2.4 %shard_map.68 = (bf16[32,8,8,128]{3,2,1,0:T(8,128)(2,1)}, f32[27,32,32]{2,1,0:T(8,128)}, f32[27,32,32]{2,1,0:T(8,128)}) custom-call(bf16[8,256,128]{2,1,0:T(8,128)(2,1)} %get-tuple-element.8.res_ref, f32[2,27,8,128]{3,2,1,0:T(8,128)} %get-tuple-element.9.sums_ref), custom_call_target="tpu_custom_call" | custom-call | tf_op jit(solution)/shard_map/pallas_call | solution.py:430
